TPU v7x, 16 devices: a 4x2x1 block of a 4x4x8 slice. The times are simulated.
16 devices in a mesh: dp: 4 (over y, z, core), ep: 4 (over x).
Axes of the slice: x: 4, y: 2, z: 1, core: 2. Of those that a mesh axis runs over, the one named last changes fastest.
The devices are a block of a 4x4x8 slice.
Arguments:
- x: bfloat16 [4, 4, 512, 2048], P('dp', 'ep'), parts along dimension 0
- expert: int32 [4, 4, 512, 8], P('dp', 'ep'), parts along dimension 0
- slot: int32 [4, 4, 512, 8], P('dp', 'ep'), parts along dimension 0
- gate: float32 [4, 4, 512, 8], P('dp', 'ep'), parts along dimension 0
- w_gate: bfloat16 [64, 2048, 1024], P('ep')
- w_up: bfloat16 [64, 2048, 1024], P('ep')
- w_down: bfloat16 [64, 1024, 2048], P('ep')
Outputs:
- y: bfloat16 [4, 4, 512, 2048], P('dp', 'ep'), parts along dimension 0
There are 4 independent parts. A program takes and returns all parts, laid end to end along the dimension named above; an argument that names none is the same for every part.
All inputs are finite; a program needn't handle non-finite values.
Results may differ from a plain program's by a relative error of at most 0.009.
Values are sent between devices in bfloat16 or wider.
A program may use at most 768 MiB of HBM per device.

v0:
```python
import jax
import jax.numpy as jnp
from jax import lax
from jax.sharding import NamedSharding, PartitionSpec as P


def einsum(form, a, b):
    return jnp.einsum(form, a.astype(jnp.float32), b.astype(jnp.float32))


def solution(mesh):
    def placed(v, *spec):
        return lax.with_sharding_constraint(v, NamedSharding(mesh, P(*spec)))

    def step(x, expert, slot, gate, w_gate, w_up, w_down):
        experts, (tokens, top) = w_gate.shape[0], expert.shape[2:]
        slots = 5 * tokens * top // (4 * experts)
        to_expert = jax.nn.one_hot(expert, experts, dtype=jnp.bfloat16)
        to_slot = jax.nn.one_hot(slot, slots, dtype=jnp.bfloat16)
        weighted = to_expert * gate[..., None].astype(jnp.bfloat16)
        dispatch = einsum("abtke,abtkc->abtec", to_expert, to_slot).astype(jnp.bfloat16)
        combine = einsum("abtke,abtkc->abtec", weighted, to_slot).astype(jnp.bfloat16)
        z = einsum("abtec,abtd->aebcd", dispatch, x).astype(jnp.bfloat16)
        z = placed(z, "dp", None, "ep", None, None)
        z = placed(z, "dp", "ep", None, None, None)
        h = jax.nn.silu(einsum("aebcd,edf->aebcf", z, w_gate))
        h = (h * einsum("aebcd,edf->aebcf", z, w_up)).astype(jnp.bfloat16)
        out = einsum("aebcf,efd->aebcd", h, w_down).astype(jnp.bfloat16)
        out = placed(out, "dp", "ep", None, None, None)
        out = placed(out, "dp", None, "ep", None, None)
        y = einsum("abtec,aebcd->abtd", combine, out)
        return y.astype(jnp.bfloat16)

    return step
```

profile of v0, /device:TPU:112, one launch (start us, length us, event | category | flops | bytes accessed | tf_op | source)
XLA Modules:
  0.0 741.2 jit_solution(15289530786888959932)
XLA Ops:
  0.0 0.0 copy-start
  0.0 1.0 copy.11
  1.0 0.0 copy-start.2
  1.0 0.9 copy.9
  1.9 0.0 copy-start.4
  1.9 8.1 %convolution_convert_fusion.1 = bf16[512,64,80]{2,1,0:T(8,128)(2,1)} fusion(s32[512,8]{1,0:T(8,128)S(1)} %copy.11, s32[512,8]{1,0:T(8,128)S(1)} %copy.9), kind=kOutput, calls=%fused_computation.23 | convolution fusion | flops 45154304 | bytes 5275648 | tf_op jit(solution)/abtke,abtkc->abtec/dot_general | solution.py:8
  10.0 0.0 copy-done
  10.0 79.9 %convolution_convert_fusion = bf16[64,80,2048]{2,1,0:T(8,128)(2,1)} fusion(bf16[512,64,80]{2,1,0:T(8,128)(2,1)} %convolution_convert_fusion.1, bf16[1,1,512,2048]{3,2,1,0:T(8,128)(2,1)S(1)} %copy-done), kind=kOutput, calls=%fused_computation.18 | convolution fusion | flops 10747904000 | bytes 28311552 | tf_op jit(solution)/abtec,abtd->aebcd/dot_general | solution.py:8
  90.0 0.0 copy-done.2
  90.0 0.0 copy-done.4
  90.0 242.3 %all-to-all.4 = bf16[1,4,16,1,80,2048]{5,4,2,3,0,1:T(8,128)(2,1)} all-to-all(bf16[1,4,16,1,80,2048]{5,4,2,3,0,1:T(8,128)(2,1)} %bitcast.84), channel_id=1, replica_groups=mesh['dp'=4,'ep'=4] {'ep'}, dimensions={1} | all-to-all | bytes 41943040 | tf_op jit(solution)/sharding_constraint;jit(solution)/sharding_constraint | solution.py:13
  332.3 41.3 %fusion.2 = f32[16,4,80,1024]{3,2,1,0:T(8,128)} fusion(bf16[16,2048,1024]{2,1,0:T(8,128)(2,1)} %param.5, bf16[1,4,16,1,80,2048]{5,4,2,3,0,1:T(8,128)(2,1)} %all-to-all.4), kind=kOutput, calls=%fused_computation.2 | convolution fusion | flops 21474836480 | bytes 109051904 | tf_op jit(solution)/aebcd,edf->aebcf/dot_general | solution.py:8
  373.6 42.4 %fusion.6 = bf16[1,16,4,80,1024]{4,3,2,1,0:T(8,128)(2,1)} fusion(f32[16,4,80,1024]{3,2,1,0:T(8,128)} %fusion.2, bf16[16,2048,1024]{2,1,0:T(8,128)(2,1)} %param.4, bf16[1,4,16,1,80,2048]{5,4,2,3,0,1:T(8,128)(2,1)} %all-to-all.4), kind=kOutput, calls=%fused_computation.7 | convolution fusion | flops 21506293760 | bytes 119537664 | tf_op jit(solution)/aebcd,edf->aebcf/dot_general | solution.py:8
  416.0 38.2 %convert_bitcast_fusion = bf16[1,16,4,1,80,2048]{5,4,2,1,3,0:T(8,128)(2,1)} fusion(bf16[16,1024,2048]{2,1,0:T(8,128)(2,1)} %param.6, bf16[1,16,4,80,1024]{4,3,2,1,0:T(8,128)(2,1)} %fusion.6), kind=kOutput, calls=%fused_computation.15 | convolution fusion | flops 21485322240 | bytes 98566144 | tf_op jit(solution)/aebcf,efd->aebcd/dot_general | solution.py:8
  454.3 17.6 %copy.15 = bf16[1,16,4,1,80,2048]{5,4,1,3,0,2:T(8,128)(2,1)} copy(bf16[1,16,4,1,80,2048]{5,4,2,1,3,0:T(8,128)(2,1)} %convert_bitcast_fusion) | data formatting | bytes 41943040 | tf_op jit(solution)/sharding_constraint;jit(solution)/sharding_constraint | solution.py:13
  471.9 0.0 copy-start.6
  471.9 0.0 copy-start.3
  471.9 0.0 copy-start.5
  471.9 8.0 %all-to-all-start.1 = ((bf16[1,16,4,1,80,2048]{5,4,1,3,0,2:T(8,128)(2,1)}), bf16[1,16,4,1,80,2048]{5,4,1,3,0,2:T(8,128)(2,1)}, u32[]{:S(2)}, u32[]{:S(2)}) async-start(bf16[1,16,4,1,80,2048]{5,4,1,3,0,2:T(8,128)(2,1)} %copy.15), calls=%async_computation.1 | async-start | bytes 41943040 | tf_op jit(solution)/sharding_constraint;jit(solution)/sharding_constraint | solution.py:13
  479.9 0.0 copy-done.6
  479.9 0.2 copy.10
  480.1 0.0 copy-done.3
  480.1 0.0 copy-done.5
  480.1 8.8 %convolution_convert_fusion.2 = bf16[512,64,80]{2,1,0:T(8,128)(2,1)} fusion(s32[512,8]{1,0:T(8,128)S(1)} %copy-done.3, s32[512,8]{1,0:T(8,128)S(1)} %copy-done.5, bf16[512,8]{1,0:T(8,128)(2,1)S(1)} %copy.10), kind=kOutput, calls=%fused_computation.24 | convolution fusion | flops 45416448 | bytes 5283840 | tf_op jit(solution)/abtke,abtkc->abtec/dot_general | solution.py:8
  488.9 219.1 %all-to-all-done.1 = bf16[1,16,4,1,80,2048]{5,4,1,3,0,2:T(8,128)(2,1)} async-done(((bf16[1,16,4,1,80,2048]{5,4,1,3,0,2:T(8,128)(2,1)}), bf16[1,16,4,1,80,2048]{5,4,1,3,0,2:T(8,128)(2,1)}, u32[]{:S(2)}, u32[]{:S(2)}) %all-to-all-start.1) | async-done | bytes 20971552 | tf_op jit(solution)/sharding_constraint;jit(solution)/sharding_constraint | solution.py:13
  708.0 0.0 copy-start.1
  708.0 32.9 %fusion.26 = bf16[1,1,512,2048]{3,2,1,0:T(8,128)(2,1)} fusion(bf16[64,80,2048]{2,1,0:T(8,128)(2,1)} %bitcast.25, bf16[512,64,80]{2,1,0:T(8,128)(2,1)} %convolution_convert_fusion.2), kind=kOutput, calls=%fused_computation.26 | convolution fusion | flops 10738466816 | bytes 28311552 | tf_op jit(solution)/abtec,aebcd->abtd/dot_general | solution.py:8
  740.9 0.0 copy-done.1
  (1 shorter events, 0.0 us)
Async XLA Ops:
  0.0 10.0 %copy-start = (bf16[1,1,512,2048]{3,2,1,0:T(8,128)(2,1)S(1)}, bf16[1,1,512,2048]{3,2,1,0:T(8,128)(2,1)}, u32[]{:S(2)}) copy-start(bf16[1,1,512,2048]{3,2,1,0:T(8,128)(2,1)} %param.3) | copy-start | bytes 6291460
  1.0 89.0 %copy-start.2 = (s32[512,8]{1,0:T(8,128)}, s32[512,8]{1,0:T(8,128)S(1)}, u32[]{:S(2)}) copy-start(s32[512,8]{1,0:T(8,128)S(1)} %copy.11) | copy-start | bytes 49156
  1.9 88.1 %copy-start.4 = (s32[512,8]{1,0:T(8,128)}, s32[512,8]{1,0:T(8,128)S(1)}, u32[]{:S(2)}) copy-start(s32[512,8]{1,0:T(8,128)S(1)} %copy.9) | copy-start | bytes 49156
  471.9 8.0 %copy-start.6 = (f32[1,1,512,8]{2,3,1,0:T(8,128)S(1)}, f32[1,1,512,8]{2,3,1,0:T(8,128)}, u32[]{:S(2)}) copy-start(f32[1,1,512,8]{2,3,1,0:T(8,128)} %param.1) | copy-start | bytes 49156
  471.9 8.2 %copy-start.3 = (s32[512,8]{1,0:T(8,128)S(1)}, s32[512,8]{1,0:T(8,128)}, u32[]{:S(2)}) copy-start(s32[512,8]{1,0:T(8,128)} %copy-done.2) | copy-start | bytes 49156
  471.9 8.2 %copy-start.5 = (s32[512,8]{1,0:T(8,128)S(1)}, s32[512,8]{1,0:T(8,128)}, u32[]{:S(2)}) copy-start(s32[512,8]{1,0:T(8,128)} %copy-done.4) | copy-start | bytes 49156
  471.9 236.1 %all-to-all-start.1 = ((bf16[1,16,4,1,80,2048]{5,4,1,3,0,2:T(8,128)(2,1)}), bf16[1,16,4,1,80,2048]{5,4,1,3,0,2:T(8,128)(2,1)}, u32[]{:S(2)}, u32[]{:S(2)}) async-start(bf16[1,16,4,1,80,2048]{5,4,1,3,0,2:T(8,128)(2,1)} %copy.15), calls=%async_computation.1 | async-start | bytes 41943040 | tf_op jit(solution)/sharding_constraint;jit(solution)/sharding_constraint | solution.py:13
  708.0 32.9 %copy-start.1 = (bf16[1,1,512,2048]{3,2,1,0:T(8,128)(2,1)S(1)}, bf16[1,1,512,2048]{3,2,1,0:T(8,128)(2,1)}, u32[]{:S(2)}) copy-start(bf16[1,1,512,2048]{3,2,1,0:T(8,128)(2,1)} %param.3) | copy-start | bytes 6291460
where the time goes:
time: 744 us; the launch traced here: 741 us
  matrix products  252 us (34%)
  blocking collectives  242 us (33%)
  waiting for transfers between devices  219 us (29%)
  local copies, waits for them, and re-layouts  19.6 us (3%)
  starting transfers between devices  7.96 us (1%)
    dot_general x7, matrix products, einsum(): return jnp.einsum(form, a.astype(jnp.float32), b.astype(jnp.float32))  252 us
    another operation x1, blocking collectives, placed(): return lax.with_sharding_constraint(v, NamedSharding(mesh, P(*spec)))  242 us
    another operation x1, waiting for transfers between devices, placed(): return lax.with_sharding_constraint(v, NamedSharding(mesh, P(*spec)))  219 us
    another operation x1, local copies, waits for them, and re-layouts, placed(): return lax.with_sharding_constraint(v, NamedSharding(mesh, P(*spec)))  17.6 us
  transfers between devices with their start and end apart: 1, of which 1 were waited for; matrix products, arithmetic and copies ran while one was open for 1% of the time, Pallas kernels for 0%

commit v1 on v0

v1 whole, which is shorter than its diff:
```python
import functools

import jax
import jax.numpy as jnp
from jax import lax
from jax.experimental import pallas as pl
from jax.experimental.pallas import tpu as pltpu
from jax.sharding import PartitionSpec as P

BF = jnp.bfloat16
F32 = jnp.float32
BC = 256
NB = 8


def dot(a, b):
    return jnp.dot(a, b, preferred_element_type=F32)


def kernel(
    n, el, cap, x_ref, meta_ref, wg_ref, wu_ref, wd_ref,
    y_ref, xg_ref, ro_ref, rl_ref,
    acc_g, acc_u, dmat, wmat, xbuf, zbuf, wbuf, so_buf, sl_buf, st_o, st_l, ybuf, meta, sg,
    wsem, xsem, xs_send, xs_recv, m_send, m_recv, o_send, o_recv, l_send, l_recv, st_sem, y_sem,
):
    tokens, d = x_ref.shape
    ff = wg_ref.shape[2]
    nc = d // BC
    half = tokens // 2
    rows = n * cap
    per = el * cap
    me = lax.axis_index("ep")
    right, left, opp = lax.rem(me + 1, n), lax.rem(me + n - 1, n), lax.rem(me + 2, n)
    tiles1 = nc * el * 2
    tiles = tiles1 + nc * el


    def start_gu(c, e, which):
        q = c * (2 * el) + 2 * e + which
        s = lax.rem(q, NB)
        w = (wg_ref, wu_ref)[which]
        for j in range(ff // BC):
            pltpu.make_async_copy(
                w.at[e, pl.ds(c * BC, BC), pl.ds(j * BC, BC)], wbuf.at[s, pl.ds(j * BC, BC)], wsem.at[s]
            ).start()

    def start_dn(c, e):
        s = lax.rem(tiles1 + c * el + e, NB)
        pltpu.make_async_copy(wd_ref.at[e, :, pl.ds(c * BC, BC)], wbuf.at[s], wsem.at[s]).start()

    def start_tile(q, which):
        @pl.when(q < tiles1)
        def _():
            c = q // (2 * el)
            start_gu(c, lax.rem(q, 2 * el) // 2, which)

        @pl.when(jnp.logical_and(q >= tiles1, q < tiles))
        def _():
            r = q - tiles1
            start_dn(r // el, lax.rem(r, el))

    def wait_tile(q):
        s = lax.rem(q, NB)
        pltpu.make_async_copy(wbuf.at[s], wbuf.at[s], wsem.at[s]).wait()
        return s

    for q in range(NB):
        start_tile(q, q % 2)

    def load_own(c):
        return pltpu.make_async_copy(x_ref.at[:, pl.ds(c * BC, BC)], xbuf.at[lax.rem(c, 2), 0], xsem.at[0])

    load_own(0).start()

    def send(src, dst, ss, rs, to):
        return pltpu.make_async_remote_copy(
            src_ref=src, dst_ref=dst, send_sem=ss, recv_sem=rs, device_id={"ep": to},
            device_id_type=pl.DeviceIdType.MESH,
        )

    def own(c, direction, part):
        h = part if direction == 0 else 1 - part
        i = 2 * direction + part
        return send(
            x_ref.at[pl.ds(h * half, half), pl.ds(c * BC, BC)],
            xg_ref.at[direction, c, pl.ds(h * half, half)],
            xs_send.at[i, c], xs_recv.at[i, c], (right, left)[direction],
        )

    def forward(c, direction):
        h = direction
        return send(
            xg_ref.at[direction, c, pl.ds(h * half, half)],
            xg_ref.at[2, c, pl.ds(h * half, half)],
            xs_send.at[4 + direction, c], xs_recv.at[4 + direction, c], (right, left)[direction],
        )

    def service(c):
        @pl.when(c < nc)
        def _():
            for direction in range(2):
                own(c, direction, 0).wait_recv()
                forward(c, direction).start()

        @pl.when(c + 1 < nc)
        def _():
            for direction in range(2):
                own(c + 1, direction, 1).start()

        @pl.when(c + 2 < nc)
        def _():
            for direction in range(2):
                own(c + 2, direction, 0).start()

    barrier = pltpu.get_barrier_semaphore()
    for to in (left, right, opp):
        pl.semaphore_signal(barrier, inc=1, device_id={"ep": to}, device_id_type=pl.DeviceIdType.MESH)
    pl.semaphore_wait(barrier, 3)

    metas = [
        send(meta_ref, meta.at[1 + i], m_send.at[i], m_recv.at[i], to) for i, to in enumerate((right, left, opp))
    ]
    for m in metas:
        m.start()
    for direction in range(2):
        own(0, direction, 0).start()
    for direction in range(2):
        own(0, direction, 1).start()
    if nc > 1:
        for direction in range(2):
            own(1, direction, 0).start()

    def clear(i, _):
        acc_g[i] = jnp.zeros(acc_g.shape[1:], F32)
        acc_u[i] = jnp.zeros(acc_u.shape[1:], F32)
        return 0

    meta[0] = meta_ref[...]
    lax.fori_loop(0, el, clear, 0)

    top = meta_ref.shape[0] // 2
    base = (me * per).astype(F32)
    first = lax.broadcasted_iota(jnp.int32, (el, tokens), 0).astype(F32) * cap + base
    line = lax.broadcasted_iota(jnp.int32, (cap, tokens), 0).astype(F32)

    def build(b, _):
        @pl.when(b == 1)
        def _():
            for m in metas:
                m.wait_recv()

        s = jnp.full((el, tokens), -1.0, F32)
        g = jnp.zeros((el, tokens), F32)
        for k in range(top):
            r = meta[b, pl.ds(k, 1)] - first
            ok = jnp.logical_and(r >= 0.0, r < cap)
            s = jnp.where(ok, r, s)
            g = jnp.where(ok, meta[b, pl.ds(top + k, 1)], g)
        sg[0] = s
        sg[1] = g

        def lines(e, _):
            eq = sg[0, pl.ds(e, 1)] == line
            at = pl.multiple_of(e * cap, 16)
            dmat[b, pl.ds(at, cap)] = jnp.where(eq, 1.0, 0.0).astype(BF)
            w = jnp.where(eq, sg[1, pl.ds(e, 1)], 0.0).astype(BF)
            for j in range(tokens // BC):
                zbuf[pl.ds(pl.multiple_of(j * per + e * cap, 16), cap)] = w[:, j * BC : (j + 1) * BC]
            return 0

        lax.fori_loop(0, el, lines, 0)
        for i in range(per // 128):
            for j in range(tokens // BC):
                t = zbuf[pl.ds(j * per + i * 128, 128)]
                wmat[b, pl.ds(j * BC, BC), pl.ds(i * 128, 128)] = t.T
        return 0

    lax.fori_loop(0, n, build, 0)
    service(0)

    def gate_up(c, p, last):
        for u in range(2):
            e = 2 * p + u
            q = c * (2 * el) + 2 * e
            z = zbuf[pl.ds(pl.multiple_of(e * rows, 16), rows)]
            sa = wait_tile(q)
            sb = wait_tile(q + 1)
            for j in range(ff // BC):
                cols = pl.ds(j * BC, BC)
                g = acc_g[e, :, cols] + dot(z, wbuf[sa, cols])
                v = acc_u[e, :, cols] + dot(z, wbuf[sb, cols])
                if last:
                    acc_g[e, :, cols] = (g * jax.nn.sigmoid(g) * v).astype(BF).astype(F32)
                else:
                    acc_g[e, :, cols] = g
                    acc_u[e, :, cols] = v
            start_tile(q + NB, 0)
            start_tile(q + NB + 1, 1)

    def phase1(c, last):
        slot = lax.rem(c, 2)
        for direction in range(2):
            own(c, direction, 1).wait_recv()
        loads = [
            pltpu.make_async_copy(xg_ref.at[i, c], xbuf.at[slot, 1 + i], xsem.at[1 + i]) for i in range(3)
        ]
        loads[0].start()
        loads[1].start()
        for direction in range(2):
            forward(c, direction).wait_recv()
        loads[2].start()
        for b in range(n):
            if b == 0:
                load_own(c).wait()
            else:
                loads[b - 1].wait()
            z = dot(dmat[b], xbuf[slot, b]).astype(BF)
            for e in range(el):
                zbuf[pl.ds(e * rows + b * cap, cap)] = z[e * cap : (e + 1) * cap]
        if not last:
            load_own(c + 1).start()

        def body(p, _):
            gate_up(c, p, last)
            return 0

        lax.fori_loop(0, el // 4, body, 0)
        if not last:
            service(c + 1)
        lax.fori_loop(el // 4, el // 2, body, 0)

    def loop1(c, _):
        phase1(c, False)
        return 0

    lax.fori_loop(0, nc - 1, loop1, 0)
    phase1(nc - 1, True)

    def keep(kind, c, value):
        for i in range(2):
            acc_u[2 * c + i, pl.ds(0, half), pl.ds(kind * BC, BC)] = value[i * half : (i + 1) * half]

    def kept(kind, c, i):
        return acc_u[2 * c + i, pl.ds(0, half), pl.ds(kind * BC, BC)]

    def send_o(c, i):
        slot = lax.rem(c, 2)
        return send(
            so_buf.at[slot, pl.ds(i * half, half)], ro_ref.at[c, i], o_send.at[i, slot], o_recv.at[i, c],
            (left, right)[i],
        )

    def send_l(c, i):
        slot = lax.rem(c, 2)
        return send(
            sl_buf.at[slot, i], rl_ref.at[c, i], l_send.at[i, slot], l_recv.at[i, c], (left, right)[i]
        )

    def stage_o(c):
        return pltpu.make_async_copy(ro_ref.at[c], st_o, st_sem.at[0])

    def stage_l(c):
        return pltpu.make_async_copy(rl_ref.at[c], st_l, st_sem.at[1])

    def out_y(c):
        slot = lax.rem(c, 2)
        return pltpu.make_async_copy(ybuf.at[slot], y_ref.at[:, pl.ds(c * BC, BC)], y_sem.at[slot])

    def arrive_o(c):
        for i in range(2):
            send_o(c, i).wait_recv()
        stage_o(c).start()

    def arrive_l(c):
        for i in range(2):
            send_l(c, i).wait_recv()
        stage_l(c).start()

    def pass_on(c):
        stage_o(c).wait()
        slot = lax.rem(c, 2)

        @pl.when(c >= 2)
        def _():
            for i in range(2):
                send_l(c - 2, i).wait_send()

        for i in range(2):
            sl_buf[slot, i, pl.ds(i * half, half)] = (kept(1 + i, c, i) + st_o[i].astype(F32)).astype(BF)
            sl_buf[slot, i, pl.ds((1 - i) * half, half)] = kept(1 + i, c, 1 - i).astype(BF)
            send_l(c, i).start()

    def finish(c):
        stage_l(c).wait()
        slot = lax.rem(c, 2)

        @pl.when(c >= 2)
        def _():
            out_y(c - 2).wait()

        for i in range(2):
            r = pl.ds(i * half, half)
            ybuf[slot, r] = (kept(0, c, i) + st_l[0, r].astype(F32) + st_l[1, r].astype(F32)).astype(BF)
        out_y(c).start()

    def phase2(c, _):
        def down(p, _):
            for u in range(2):
                e = 2 * p + u
                q = tiles1 + c * el + e
                s = wait_tile(q)
                o = dot(acc_g[e].astype(BF), wbuf[s]).astype(BF)
                for b in range(n):
                    zbuf[pl.ds(pl.multiple_of(b * per + e * cap, 16), cap)] = o[b * cap : (b + 1) * cap]
                start_tile(q + NB, u)
            return 0

        lax.fori_loop(0, el // 4, down, 0)

        @pl.when(c >= 1)
        def _():
            arrive_o(c - 1)

        @pl.when(c >= 2)
        def _():
            arrive_l(c - 2)

        lax.fori_loop(el // 4, el // 2, down, 0)

        slot = lax.rem(c, 2)

        @pl.when(c >= 2)
        def _():
            for i in range(2):
                send_o(c - 2, i).wait_send()

        so_buf[slot] = dot(wmat[3], zbuf[pl.ds(3 * per, per)]).astype(BF)
        for i in range(2):
            send_o(c, i).start()

        @pl.when(c >= 1)
        def _():
            pass_on(c - 1)

        for kind in range(3):
            keep(kind, c, dot(wmat[kind], zbuf[pl.ds(kind * per, per)]))

        @pl.when(c >= 2)
        def _():
            finish(c - 2)

        return 0

    lax.fori_loop(0, nc, phase2, 0)
    arrive_o(nc - 1)
    pass_on(nc - 1)
    for c in (nc - 2, nc - 1):
        arrive_l(c)
        finish(c)
    for c in (nc - 2, nc - 1):
        out_y(c).wait()
        for i in range(2):
            send_o(c, i).wait_send()
            send_l(c, i).wait_send()

    def drain(c, _):
        for direction in range(2):
            for part in range(2):
                own(c, direction, part).wait_send()
            forward(c, direction).wait_send()
        return 0

    lax.fori_loop(0, nc, drain, 0)
    for m in metas:
        m.wait_send()


def solution(mesh):
    n = mesh.shape["ep"]

    def step(x, expert, slot, gate, w_gate, w_up, w_down):
        x, expert, slot, gate = (v[0, 0] for v in (x, expert, slot, gate))
        tokens, d = x.shape
        el, _, ff = w_gate.shape
        top = expert.shape[1]
        cap = 5 * tokens * top // (4 * el * n)
        nc = d // BC
        half = tokens // 2
        key = jnp.where(slot < cap, expert * cap + slot, -1)
        meta = jnp.concatenate([key.astype(F32).T, gate.astype(BF).astype(F32).T], 0)
        any_, vmem = pl.BlockSpec(memory_space=pl.ANY), pl.BlockSpec(memory_space=pltpu.VMEM)
        dma = pltpu.SemaphoreType.DMA
        y, *_ = pl.pallas_call(
            functools.partial(kernel, n, el, cap),
            out_shape=[
                jax.ShapeDtypeStruct((tokens, d), BF),
                jax.ShapeDtypeStruct((n - 1, nc, tokens, BC), BF),
                jax.ShapeDtypeStruct((nc, 2, half, BC), BF),
                jax.ShapeDtypeStruct((nc, 2, tokens, BC), BF),
            ],
            in_specs=[any_, vmem, any_, any_, any_],
            out_specs=[any_] * 4,
            scratch_shapes=[
                pltpu.VMEM((el, n * cap, ff), F32),
                pltpu.VMEM((el, n * cap, ff), F32),
                pltpu.VMEM((n, el * cap, tokens), BF),
                pltpu.VMEM((n, tokens, el * cap), BF),
                pltpu.VMEM((2, n, tokens, BC), BF),
                pltpu.VMEM((n * el * cap, BC), BF),
                pltpu.VMEM((NB, ff, BC), BF),
                pltpu.VMEM((2, tokens, BC), BF),
                pltpu.VMEM((2, 2, tokens, BC), BF),
                pltpu.VMEM((2, half, BC), BF),
                pltpu.VMEM((2, tokens, BC), BF),
                pltpu.VMEM((2, tokens, BC), BF),
                pltpu.VMEM((n, 2 * top, tokens), F32),
                pltpu.VMEM((2, el, tokens), F32),
                dma((NB,)),
                dma((n,)),
                dma((6, nc)),
                dma((6, nc)),
                dma((3,)),
                dma((3,)),
                dma((2, 2)),
                dma((2, nc)),
                dma((2, 2)),
                dma((2, nc)),
                dma((2,)),
                dma((2,)),
            ],
            compiler_params=pltpu.CompilerParams(
                collective_id=0, has_side_effects=True, vmem_limit_bytes=67043328
            ),
        )(x, meta, w_gate, w_up, w_down)
        return y[None, None]

    token, weight = P("dp", "ep", None, None), P("ep", None, None)
    return jax.shard_map(
        step,
        mesh=mesh,
        in_specs=(token,) * 4 + (weight,) * 3,
        out_specs=token,
        check_vma=False,
    )
```

time: 744 us -> 234 us (0.31)
  matrix products: 252 us -> 0 us
  blocking collectives: 242 us -> 0 us
  Pallas kernels: 0 us -> 228 us
  waiting for transfers between devices: 219 us -> 0 us
  local copies, waits for them, and re-layouts: 19.6 us -> 3.16 us
  starting transfers between devices: 7.96 us -> 0 us
    dot_general x7 -> x0, matrix products: 252 us -> none  [einsum(): return jnp.einsum(form, a.astype(jnp.float32), b.astype(jnp.float32))]
    another operation x1 -> x0, blocking collectives: 242 us -> none  [placed(): return lax.with_sharding_constraint(v, NamedSharding(mesh, P(*spec)))]
    pallas_call x0 -> x1, Pallas kernels: none -> 228 us  [step(): pl.pallas_call(functools.partial(kernel, n, el, cap), out_shape=[jax.Shap...]
    another operation x1 -> x0, waiting for transfers between devices: 219 us -> none  [placed(): return lax.with_sharding_constraint(v, NamedSharding(mesh, P(*spec)))]
    another operation x1 -> x0, local copies, waits for them, and re-layouts: 17.6 us -> none  [placed(): return lax.with_sharding_constraint(v, NamedSharding(mesh, P(*spec)))]
    another operation x1 -> x0, starting transfers between devices: 7.96 us -> none  [placed(): return lax.with_sharding_constraint(v, NamedSharding(mesh, P(*spec)))]
  transfers between devices with their start and end apart: 1 -> 0, of which waited for: 1 -> 0; matrix products, arithmetic and copies ran while one was open for 1% -> 0% of each run, Pallas kernels for 0% -> 0%
where the time goes in v1:
time: 234 us; the launch traced here: 233 us
  Pallas kernels  228 us (97%)
  local copies, waits for them, and re-layouts  3.16 us (1%)
    pallas_call x1, Pallas kernels, step(): pl.pallas_call(functools.partial(kernel, n, el, cap), out_shape=[jax.Shap...  228 us

profile of v1, /device:TPU:112, one launch (start us, length us, event | category | flops | bytes accessed | tf_op | source)
XLA Modules:
  0.0 233.2 jit_solution(1931647879412927529)
XLA Ops:
  0.0 0.7 convert_bitcast_fusion.1
  0.7 0.7 convert_bitcast_fusion
  1.5 0.6 pad_maximum_fusion.meta_ref
  2.1 227.9 %shard_map.73 = (bf16[512,2048]{1,0:T(8,128)(2,1)}, bf16[3,8,512,256]{3,2,1,0:T(8,128)(2,1)}, bf16[8,2,256,256]{3,2,1,0:T(8,128)(2,1)}, bf16[8,2,512,256]{3,2,1,0:T(8,128)(2,1)}) custom-call(bf16[512,2048]{1,0:T(8,128)(2,1)} %bitcast.11, f32[16,512]{1,0:T(8,128)} %pad_maximum_fusion.meta_ref, bf16[16,2048,1024]{2,1,0:T(8,128)(2,1)} %wg_ref.1, ...), custom_call_target="tpu_custom_call" | custom-call | tf_op jit(solution)/shard_map/pallas_call | solution.py:393
  230.0 3.2 %copy.9 = bf16[1,1,512,2048]{3,2,1,0:T(8,128)(2,1)} copy(bf16[1,1,512,2048]{3,2,1,0:T(8,128)(2,1)} %bitcast.12) | data formatting | bytes 4194304

commit v2 on v1

v2 whole, which is shorter than its diff:
```python
import functools

import jax
import jax.numpy as jnp
from jax import lax
from jax.experimental import pallas as pl
from jax.experimental.pallas import tpu as pltpu
from jax.sharding import PartitionSpec as P

BF = jnp.bfloat16
F32 = jnp.float32
BC = 256
NB = 12
NX = 4


def dot(a, b):
    return jnp.dot(a, b, preferred_element_type=F32)


def kernel(
    n, el, cap, x_ref, meta_ref, wg_ref, wu_ref, wd_ref,
    y_ref, rl_ref,
    acc_g, acc_u, dmat, wmat, xbuf, zbuf, wbuf, ybuf, meta,
    wsem, xsem, xs_send, xs_recv, m_send, m_recv, o_send, o_recv, l_send, l_recv, st_sem, y_sem, credit,
):
    tokens, d = x_ref.shape
    ff = wg_ref.shape[2]
    nc = d // BC
    half = tokens // 2
    rows = n * cap
    per = el * cap
    me = lax.axis_index("ep")
    right, left, opp = lax.rem(me + 1, n), lax.rem(me + n - 1, n), lax.rem(me + 2, n)
    tiles1 = nc * el * 2


    def start_gu(c, e):
        for i, w in enumerate((wg_ref, wu_ref)):
            s = lax.rem(c * (2 * el) + 2 * e + i, NB)
            pltpu.make_async_copy(w.at[e, pl.ds(c * BC, BC)], wbuf.at[s], wsem.at[s]).start()

    def start_dn(c, e):
        s = lax.rem(tiles1 + c * el + e, NB)
        for j in range(ff // BC):
            pltpu.make_async_copy(
                wd_ref.at[e, pl.ds(j * BC, BC), pl.ds(c * BC, BC)], wbuf.at[s, :, pl.ds(j * BC, BC)], wsem.at[s]
            ).start()

    def wait_tile(q):
        s = lax.rem(q, NB)
        pltpu.make_async_copy(wbuf.at[s], wbuf.at[s], wsem.at[s]).wait()
        return s

    for e in range(NB // 2):
        start_gu(0, e)

    def load_own(c):
        return pltpu.make_async_copy(x_ref.at[:, pl.ds(c * BC, BC)], xbuf.at[lax.rem(c, NX), 0], xsem.at[lax.rem(c, NX)])


    for c in range(NX):
        load_own(c).start()

    def send(src, dst, ss, rs, to):
        return pltpu.make_async_remote_copy(
            src_ref=src, dst_ref=dst, send_sem=ss, recv_sem=rs, device_id={"ep": to},
            device_id_type=pl.DeviceIdType.MESH,
        )

    def own(c, direction, part):
        h = part if direction == 0 else 1 - part
        i = 2 * direction + part
        return send(
            xbuf.at[lax.rem(c, NX), 0, pl.ds(h * half, half)],
            xbuf.at[lax.rem(c, NX), 1 + direction, pl.ds(h * half, half)],
            xs_send.at[i, c], xs_recv.at[i, c], (right, left)[direction],
        )

    def forward(c, direction):
        h = direction
        return send(
            xbuf.at[lax.rem(c, NX), 1 + direction, pl.ds(h * half, half)],
            xbuf.at[lax.rem(c, NX), 3, pl.ds(h * half, half)],
            xs_send.at[4 + direction, c], xs_recv.at[4 + direction, c], (right, left)[direction],
        )

    def both(c, part):
        for direction in range(2):
            own(c, direction, part).start()

    def service(c, again):
        @pl.when(c < nc)
        def _():
            for direction in range(2):
                own(c, direction, 0).wait_recv()
                forward(c, direction).start()

        @pl.when(c + 1 < nc)
        def _():
            both(c + 1, 1)

        @pl.when(c + 2 < nc)
        def _():
            if again:
                load_own(c + 2).wait()
                for direction in range(2):
                    pl.semaphore_wait(credit.at[direction], 1)
            both(c + 2, 0)

    barrier = pltpu.get_barrier_semaphore()
    for to in (left, right, opp):
        pl.semaphore_signal(barrier, inc=1, device_id={"ep": to}, device_id_type=pl.DeviceIdType.MESH)
    pl.semaphore_wait(barrier, 3)

    metas = [
        send(meta_ref, meta.at[1 + i], m_send.at[i], m_recv.at[i], to) for i, to in enumerate((right, left, opp))
    ]
    for m in metas:
        m.start()
    load_own(0).wait()
    both(0, 0)
    both(0, 1)
    meta[0] = meta_ref[...]

    top = meta_ref.shape[0] // 2
    base = (me * per).astype(F32)
    first = lax.broadcasted_iota(jnp.int32, (el, tokens), 0).astype(F32) * cap + base
    line = lax.broadcasted_iota(jnp.int32, (cap, tokens), 0).astype(F32)

    def build(b, _):
        @pl.when(b == 1)
        def _():
            for m in metas:
                m.wait_recv()

        s = jnp.full((el, tokens), -1.0, F32)
        g = jnp.zeros((el, tokens), F32)
        for k in range(top):
            r = meta[b, pl.ds(k, 1)] - first
            ok = jnp.logical_and(r >= 0.0, r < cap)
            s = jnp.where(ok, r, s)
            g = jnp.where(ok, meta[b, pl.ds(top + k, 1)], g)
        acc_u[0, pl.ds(0, el), pl.ds(0, tokens)] = s
        acc_u[1, pl.ds(0, el), pl.ds(0, tokens)] = g

        def lines(e, _):
            eq = acc_u[0, pl.ds(e, 1), pl.ds(0, tokens)] == line
            at = pl.multiple_of(e * cap, 16)
            dmat[b, pl.ds(at, cap)] = jnp.where(eq, 1.0, 0.0).astype(BF)
            w = jnp.where(eq, acc_u[1, pl.ds(e, 1), pl.ds(0, tokens)], 0.0).astype(BF)
            for j in range(tokens // BC):
                zbuf[pl.ds(pl.multiple_of(j * per + e * cap, 16), cap)] = w[:, j * BC : (j + 1) * BC]
            return 0

        lax.fori_loop(0, el, lines, 0)
        for i in range(per // 128):
            for j in range(tokens // BC):
                t = zbuf[pl.ds(j * per + i * 128, 128)]
                wmat[b, pl.ds(j * BC, BC), pl.ds(i * 128, 128)] = t.T

        @pl.when(b == 0)
        def _():
            for direction in range(2):
                own(0, direction, 0).wait_recv()
                forward(0, direction).start()
            for c in range(1, NX):
                load_own(c).wait()
            both(1, 0)
            both(1, 1)
            both(2, 0)

        return 0

    lax.fori_loop(0, n, build, 0)

    def gate_up(c, p, first, last):
        q = c * (2 * el) + 4 * p
        slots = [wait_tile(q + i) for i in range(4)]
        for u in range(2):
            e = 2 * p + u
            z = zbuf[pl.ds(pl.multiple_of(e * rows, 16), rows)]
            for j in range(ff // BC):
                cols = pl.ds(j * BC, BC)
                g = dot(z, wbuf[slots[2 * u], :, cols])
                v = dot(z, wbuf[slots[2 * u + 1], :, cols])
                if not first:
                    g = acc_g[e, :, cols] + g
                    v = acc_u[e, :, cols] + v
                if last:
                    acc_g[e, :, cols] = (g * jax.nn.sigmoid(g) * v).astype(BF).astype(F32)
                else:
                    acc_g[e, :, cols] = g
                    acc_u[e, :, cols] = v
        ahead = 2 * p + NB // 2
        if last:

            @pl.when(ahead < el)
            def _():
                for u in range(2):
                    start_gu(c, ahead + u)

            @pl.when(ahead >= el)
            def _():
                for u in range(4):
                    start_dn(0, 2 * (ahead - el) + u)
        else:
            over = (ahead >= el).astype(jnp.int32)
            for u in range(2):
                start_gu(c + over, ahead + u - over * el)

    def phase1(c, first=False, last=False):
        slot = lax.rem(c, NX)
        if not (first or last):
            service(c + 1, True)
        for direction in range(2):
            own(c, direction, 1).wait_recv()
        for direction in range(2):
            forward(c, direction).wait_recv()
        for b in range(n):
            z = dot(dmat[b], xbuf[slot, b]).astype(BF)
            for e in range(el):
                zbuf[pl.ds(e * rows + b * cap, cap)] = z[e * cap : (e + 1) * cap]
        for direction in range(2):
            own(c, direction, 0).wait_send()
            own(c, direction, 1).wait_send()
            forward(c, direction).wait_send()

        def free():
            for direction, to in enumerate((left, right)):
                pl.semaphore_signal(
                    credit.at[direction], inc=1, device_id={"ep": to}, device_id_type=pl.DeviceIdType.MESH
                )

        if last:
            free()
        else:
            pl.when(c + NX < nc)(free)
        def body(p, _):
            gate_up(c, p, first, last)
            return 0

        lax.fori_loop(0, el // 4, body, 0)
        if first:
            service(c + 1, False)
        if not last:

            @pl.when(c + NX < nc)
            def _():
                load_own(c + NX).start()

        lax.fori_loop(el // 4, el // 2, body, 0)

    def loop1(c, _):
        phase1(c)
        return 0

    phase1(0, first=True)
    lax.fori_loop(1, nc - 1, loop1, 0)
    phase1(nc - 1, last=True)

    def keep(kind, c, i, value):
        acc_u[2 * c + i, pl.ds(0, half), pl.ds(kind * BC, BC)] = value

    def kept(kind, c, i):
        return acc_u[2 * c + i, pl.ds(0, half), pl.ds(kind * BC, BC)]

    def sl_at(slot, i):
        block = 2 + 2 * slot + i
        return xbuf.at[block // n, lax.rem(block, n)]

    def ro_at(c, i):
        return xbuf.at[2 + c // n, lax.rem(c, n), pl.ds(i * half, half)]

    def put_o(slot, r, value):
        xbuf[0, slot, r] = value

    def send_o(c, i):
        slot = lax.rem(c, 2)
        return send(
            xbuf.at[0, slot, pl.ds(i * half, half)], ro_at(c, i), o_send.at[i, slot], o_recv.at[i, c],
            (left, right)[i],
        )

    def send_l(c, i):
        slot = lax.rem(c, 2)
        return send(
            sl_at(slot, i), rl_ref.at[c, i], l_send.at[i, slot], l_recv.at[i, c], (left, right)[i]
        )

    def stage_l(c):
        return pltpu.make_async_copy(rl_ref.at[c], xbuf.at[1, pl.ds(2, 2)], st_sem.at[1])

    def out_y(c):
        return pltpu.make_async_copy(ybuf, y_ref.at[:, pl.ds(c * BC, BC)], y_sem.at[0])

    def arrive_o(c):
        for i in range(2):
            send_o(c, i).wait_recv()

    def arrive_l(c):
        for i in range(2):
            send_l(c, i).wait_recv()
        stage_l(c).start()

    def pass_on(c):
        slot = lax.rem(c, 2)

        @pl.when(c >= 2)
        def _():
            for i in range(2):
                send_l(c - 2, i).wait_send()

        for i in range(2):
            to = sl_at(slot, i)
            to[pl.ds(i * half, half)] = (kept(1 + i, c, i) + ro_at(c, i)[...].astype(F32)).astype(BF)
            to[pl.ds((1 - i) * half, half)] = kept(1 + i, c, 1 - i).astype(BF)
            send_l(c, i).start()

    def finish(c):
        stage_l(c).wait()

        @pl.when(c >= 1)
        def _():
            out_y(c - 1).wait()

        for i in range(2):
            r = pl.ds(i * half, half)
            ybuf[r] = (kept(0, c, i) + xbuf[1, 2, r].astype(F32) + xbuf[1, 3, r].astype(F32)).astype(BF)
        out_y(c).start()

    def phase2(c, _):
        def down(p, _):
            q = tiles1 + c * el + 4 * p
            slots = [wait_tile(q + i) for i in range(4)]
            for u in range(4):
                e = 4 * p + u
                w = jnp.concatenate([wbuf[slots[u], :, pl.ds(j * BC, BC)] for j in range(ff // BC)], axis=0)
                o = dot(acc_g[e].astype(BF), w).astype(BF)
                for b in range(n):
                    zbuf[pl.ds(pl.multiple_of(b * per + e * cap, 16), cap)] = o[b * cap : (b + 1) * cap]
            r = c * el + 4 * p + NB

            @pl.when(r < nc * el)
            def _():
                for i in range(4):
                    start_dn(r // el, lax.rem(r, el) + i)

            return 0

        lax.fori_loop(0, el // 4, down, 0)

        slot = lax.rem(c, 2)

        @pl.when(c >= 2)
        def _():
            for i in range(2):
                send_o(c - 2, i).wait_send()

        for i in range(2):
            r = pl.ds(i * half, half)
            put_o(slot, r, dot(wmat[3, r], zbuf[pl.ds(3 * per, per)]).astype(BF))
        @pl.when(c == 0)
        def _():
            for i in range(2):
                pl.semaphore_wait(credit.at[i], 1)

        for i in range(2):
            send_o(c, i).start()

        @pl.when(c >= 1)
        def _():
            arrive_o(c - 1)

        @pl.when(c >= 3)
        def _():
            arrive_l(c - 3)

        for kind in range(3):
            for i in range(2):
                keep(kind, c, i, dot(wmat[kind, pl.ds(i * half, half)], zbuf[pl.ds(kind * per, per)]))

        @pl.when(c >= 1)
        def _():
            pass_on(c - 1)

        @pl.when(c >= 3)
        def _():
            finish(c - 3)

        return 0

    lax.fori_loop(0, nc, phase2, 0)
    arrive_o(nc - 1)
    pass_on(nc - 1)
    for c in (nc - 3, nc - 2, nc - 1):
        arrive_l(c)
        finish(c)
    out_y(nc - 1).wait()
    for c in (nc - 2, nc - 1):
        for i in range(2):
            send_o(c, i).wait_send()
            send_l(c, i).wait_send()

    for m in metas:
        m.wait_send()


def solution(mesh):
    n = mesh.shape["ep"]

    def step(x, expert, slot, gate, w_gate, w_up, w_down):
        x, expert, slot, gate = (v[0, 0] for v in (x, expert, slot, gate))
        tokens, d = x.shape
        el, _, ff = w_gate.shape
        top = expert.shape[1]
        cap = 5 * tokens * top // (4 * el * n)
        nc = d // BC
        half = tokens // 2
        key = jnp.where(slot < cap, expert * cap + slot, -1)
        meta = jnp.concatenate([key.astype(F32).T, gate.astype(BF).astype(F32).T], 0)
        any_, vmem = pl.BlockSpec(memory_space=pl.ANY), pl.BlockSpec(memory_space=pltpu.VMEM)
        dma = pltpu.SemaphoreType.DMA
        y, *_ = pl.pallas_call(
            functools.partial(kernel, n, el, cap),
            out_shape=[
                jax.ShapeDtypeStruct((tokens, d), BF),
                jax.ShapeDtypeStruct((nc, 2, tokens, BC), BF),
            ],
            in_specs=[any_, vmem, any_, any_, any_],
            out_specs=[any_] * 2,
            scratch_shapes=[
                pltpu.VMEM((el, n * cap, ff), F32),
                pltpu.VMEM((el, n * cap, ff), F32),
                pltpu.VMEM((n, el * cap, tokens), BF),
                pltpu.VMEM((n, tokens, el * cap), BF),
                pltpu.VMEM((NX, n, tokens, BC), BF),
                pltpu.VMEM((n * el * cap, BC), BF),
                pltpu.VMEM((NB, BC, ff), BF),
                pltpu.VMEM((tokens, BC), BF),
                pltpu.VMEM((n, 2 * top, tokens), F32),
                dma((NB,)),
                dma((NX,)),
                dma((6, nc)),
                dma((6, nc)),
                dma((3,)),
                dma((3,)),
                dma((2, 2)),
                dma((2, nc)),
                dma((2, 2)),
                dma((2, nc)),
                dma((2,)),
                dma((1,)),
                pltpu.SemaphoreType.REGULAR((2,)),
            ],
            compiler_params=pltpu.CompilerParams(
                collective_id=0, has_side_effects=True, vmem_limit_bytes=67043328
            ),
        )(x, meta, w_gate, w_up, w_down)
        return y[None, None]

    token, weight = P("dp", "ep", None, None), P("ep", None, None)
    return jax.shard_map(
        step,
        mesh=mesh,
        in_specs=(token,) * 4 + (weight,) * 3,
        out_specs=token,
        check_vma=False,
    )
```

time: 234 us -> 176 us (0.75)
  Pallas kernels: 228 us -> 171 us
    pallas_call x1, Pallas kernels: 228 us -> 171 us  [step(): pl.pallas_call(functools.partial(kernel, n, el, cap), out_shape=[jax.Shap...]
where the time goes in v2:
time: 176 us
  Pallas kernels  171 us (97%)
  local copies, waits for them, and re-layouts  3.16 us (2%)
  other arithmetic  2.08 us (1%)
    pallas_call x1, Pallas kernels, step(): pl.pallas_call(functools.partial(kernel, n, el, cap), out_shape=[jax.Shap...  171 us

profile of v2, /device:TPU:112, one launch (start us, length us, event | category | flops | bytes accessed | tf_op | source)
XLA Modules:
  0.0 175.8 jit_solution(16830126016155908470)
XLA Ops:
  0.0 0.7 convert_bitcast_fusion.1
  0.7 0.7 convert_bitcast_fusion
  1.5 0.6 pad_maximum_fusion.meta_ref
  2.1 170.6 %shard_map.73 = (bf16[512,2048]{1,0:T(8,128)(2,1)}, bf16[8,2,512,256]{3,2,1,0:T(8,128)(2,1)}) custom-call(bf16[512,2048]{1,0:T(8,128)(2,1)} %bitcast.11, f32[16,512]{1,0:T(8,128)} %pad_maximum_fusion.meta_ref, bf16[16,2048,1024]{2,1,0:T(8,128)(2,1)} %wg_ref.1, bf16[16,2048,1024]{2,1,0:T(8,128)(2,1)} %wu_ref.1, bf16[16,1024,2048]{2,1,0:T(8,128)(2,1)} %wd_ref.1), custom_call_target="tpu_custom_call" | custom-call | tf_op jit(solution)/shard_map/pallas_call | solution.py:424
  172.7 3.2 %copy.9 = bf16[1,1,512,2048]{3,2,1,0:T(8,128)(2,1)} copy(bf16[1,1,512,2048]{3,2,1,0:T(8,128)(2,1)} %bitcast.12) | data formatting | bytes 4194304

commit v3 on v2

--- a/solution.py
+++ b/solution.py
@@ -12,6 +12,7 @@
 BC = 256
 NB = 12
 NX = 4
+PIECES = 4
 
 
 def dot(a, b):
@@ -19,10 +20,10 @@
 
 
 def kernel(
-    n, el, cap, x_ref, meta_ref, wg_ref, wu_ref, wd_ref,
-    y_ref, rl_ref,
+    n, el, cap, x_ref, expert_ref, slot_ref, gate_ref, wg_ref, wu_ref, wd_ref,
+    y_ref, rl_ref, last_ref, own_ref,
     acc_g, acc_u, dmat, wmat, xbuf, zbuf, wbuf, ybuf, meta,
-    wsem, xsem, xs_send, xs_recv, m_send, m_recv, o_send, o_recv, l_send, l_recv, st_sem, y_sem, credit,
+    wsem, xsem, xs_send, xs_recv, m_send, m_recv, o_send, o_recv, l_send, l_recv, st_sem, y_sem, own_sem, credit,
 ):
     tokens, d = x_ref.shape
     ff = wg_ref.shape[2]
@@ -52,15 +53,11 @@
         pltpu.make_async_copy(wbuf.at[s], wbuf.at[s], wsem.at[s]).wait()
         return s
 
-    for e in range(NB // 2):
-        start_gu(0, e)
-
     def load_own(c):
         return pltpu.make_async_copy(x_ref.at[:, pl.ds(c * BC, BC)], xbuf.at[lax.rem(c, NX), 0], xsem.at[lax.rem(c, NX)])
 
 
-    for c in range(NX):
-        load_own(c).start()
+    load_own(0).start()
 
     def send(src, dst, ss, rs, to):
         return pltpu.make_async_remote_copy(
@@ -108,22 +105,28 @@
                     pl.semaphore_wait(credit.at[direction], 1)
             both(c + 2, 0)
 
+    top = expert_ref.shape[0]
+    slot = slot_ref[...]
+    meta[0, pl.ds(0, top)] = jnp.where(slot < cap, expert_ref[...] * cap + slot, -1).astype(F32)
+    meta[0, pl.ds(top, top)] = gate_ref[...]
+
     barrier = pltpu.get_barrier_semaphore()
     for to in (left, right, opp):
         pl.semaphore_signal(barrier, inc=1, device_id={"ep": to}, device_id_type=pl.DeviceIdType.MESH)
     pl.semaphore_wait(barrier, 3)
 
     metas = [
-        send(meta_ref, meta.at[1 + i], m_send.at[i], m_recv.at[i], to) for i, to in enumerate((right, left, opp))
+        send(meta.at[0], meta.at[1 + i], m_send.at[i], m_recv.at[i], to) for i, to in enumerate((right, left, opp))
     ]
+    load_own(0).wait()
+    both(0, 0)
     for m in metas:
         m.start()
-    load_own(0).wait()
-    both(0, 0)
     both(0, 1)
-    meta[0] = meta_ref[...]
-
-    top = meta_ref.shape[0] // 2
+    for c in range(1, NX):
+        load_own(c).start()
+    for e in range(NB // 2):
+        start_gu(0, e)
     base = (me * per).astype(F32)
     first = lax.broadcasted_iota(jnp.int32, (el, tokens), 0).astype(F32) * cap + base
     line = lax.broadcasted_iota(jnp.int32, (cap, tokens), 0).astype(F32)
@@ -153,7 +156,7 @@
                 zbuf[pl.ds(pl.multiple_of(j * per + e * cap, 16), cap)] = w[:, j * BC : (j + 1) * BC]
             return 0
 
-        lax.fori_loop(0, el, lines, 0)
+        lax.fori_loop(0, el, lines, 0, unroll=2)
         for i in range(per // 128):
             for j in range(tokens // BC):
                 t = zbuf[pl.ds(j * per + i * 128, 128)]
@@ -215,12 +218,14 @@
             service(c + 1, True)
         for direction in range(2):
             own(c, direction, 1).wait_recv()
-        for direction in range(2):
-            forward(c, direction).wait_recv()
         for b in range(n):
-            z = dot(dmat[b], xbuf[slot, b]).astype(BF)
-            for e in range(el):
-                zbuf[pl.ds(e * rows + b * cap, cap)] = z[e * cap : (e + 1) * cap]
+            if b == 3:
+                for direction in range(2):
+                    forward(c, direction).wait_recv()
+            for i in range(2):
+                z = dot(dmat[b, pl.ds(i * (per // 2), per // 2)], xbuf[slot, b]).astype(BF)
+                for e in range(el // 2):
+                    zbuf[pl.ds((i * (el // 2) + e) * rows + b * cap, cap)] = z[e * cap : (e + 1) * cap]
         for direction in range(2):
             own(c, direction, 0).wait_send()
             own(c, direction, 1).wait_send()
@@ -240,9 +245,9 @@
             gate_up(c, p, first, last)
             return 0
 
-        lax.fori_loop(0, el // 4, body, 0)
         if first:
             service(c + 1, False)
+        lax.fori_loop(0, el // 4, body, 0)
         if not last:
 
             @pl.when(c + NX < nc)
@@ -285,7 +290,7 @@
     def send_l(c, i):
         slot = lax.rem(c, 2)
         return send(
-            sl_at(slot, i), rl_ref.at[c, i], l_send.at[i, slot], l_recv.at[i, c], (left, right)[i]
+            sl_at(slot, i), last_ref.at[i] if isinstance(c, int) and c == nc - 1 else rl_ref.at[c, i], l_send.at[i, slot], l_recv.at[i, c], (left, right)[i]
         )
 
     def stage_l(c):
@@ -293,6 +298,11 @@
 
     def out_y(c):
         return pltpu.make_async_copy(ybuf, y_ref.at[:, pl.ds(c * BC, BC)], y_sem.at[0])
+
+    def out_own(i):
+        return pltpu.make_async_copy(
+            acc_u.at[2 * (nc - 1) + i, pl.ds(0, half), pl.ds(0, BC)], own_ref.at[pl.ds(i * half, half)], own_sem.at[i]
+        )
 
     def arrive_o(c):
         for i in range(2):
@@ -391,12 +401,17 @@
         return 0
 
     lax.fori_loop(0, nc, phase2, 0)
+    for i in range(2):
+        out_own(i).start()
     arrive_o(nc - 1)
     pass_on(nc - 1)
-    for c in (nc - 3, nc - 2, nc - 1):
+    for c in (nc - 3, nc - 2):
         arrive_l(c)
         finish(c)
-    out_y(nc - 1).wait()
+    out_y(nc - 2).wait()
+    for i in range(2):
+        out_own(i).wait()
+        send_l(nc - 1, i).wait_recv()
     for c in (nc - 2, nc - 1):
         for i in range(2):
             send_o(c, i).wait_send()
@@ -404,6 +419,30 @@
 
     for m in metas:
         m.wait_send()
+
+
+def end_kernel(most_ref, last_ref, own_ref, y_ref, most, last, own, end, in_sem, out_sem, sem):
+    tokens, width = most.shape
+    lasts = [
+        pltpu.make_async_copy(last_ref, last, sem.at[0]),
+        pltpu.make_async_copy(own_ref, own, sem.at[1]),
+    ]
+    rows = [pl.ds(i * (tokens // PIECES), tokens // PIECES) for i in range(PIECES)]
+    ins = [pltpu.make_async_copy(most_ref.at[r], most.at[r], in_sem.at[i]) for i, r in enumerate(rows)]
+    outs = [pltpu.make_async_copy(most.at[r], y_ref.at[r, pl.ds(0, width)], out_sem.at[i]) for i, r in enumerate(rows)]
+    for c in lasts + ins:
+        c.start()
+    for c in lasts:
+        c.wait()
+    end[...] = (own[...] + last[0].astype(F32) + last[1].astype(F32)).astype(BF)
+    final = pltpu.make_async_copy(end, y_ref.at[:, pl.ds(width, end.shape[1])], sem.at[2])
+    final.start()
+    for i, o in zip(ins, outs):
+        i.wait()
+        o.start()
+    for o in outs:
+        o.wait()
+    final.wait()
 
 
 def solution(mesh):
@@ -416,19 +455,18 @@
         top = expert.shape[1]
         cap = 5 * tokens * top // (4 * el * n)
         nc = d // BC
-        half = tokens // 2
-        key = jnp.where(slot < cap, expert * cap + slot, -1)
-        meta = jnp.concatenate([key.astype(F32).T, gate.astype(BF).astype(F32).T], 0)
         any_, vmem = pl.BlockSpec(memory_space=pl.ANY), pl.BlockSpec(memory_space=pltpu.VMEM)
         dma = pltpu.SemaphoreType.DMA
-        y, *_ = pl.pallas_call(
+        y, _, last, own = pl.pallas_call(
             functools.partial(kernel, n, el, cap),
             out_shape=[
-                jax.ShapeDtypeStruct((tokens, d), BF),
-                jax.ShapeDtypeStruct((nc, 2, tokens, BC), BF),
+                jax.ShapeDtypeStruct((tokens, d - BC), BF),
+                jax.ShapeDtypeStruct((nc - 1, 2, tokens, BC), BF),
+                jax.ShapeDtypeStruct((2, tokens, BC), BF),
+                jax.ShapeDtypeStruct((tokens, BC), F32),
             ],
-            in_specs=[any_, vmem, any_, any_, any_],
-            out_specs=[any_] * 2,
+            in_specs=[any_, vmem, vmem, vmem, any_, any_, any_],
+            out_specs=[any_] * 4,
             scratch_shapes=[
                 pltpu.VMEM((el, n * cap, ff), F32),
                 pltpu.VMEM((el, n * cap, ff), F32),
@@ -451,12 +489,29 @@
                 dma((2, nc)),
                 dma((2,)),
                 dma((1,)),
+                dma((2,)),
                 pltpu.SemaphoreType.REGULAR((2,)),
             ],
             compiler_params=pltpu.CompilerParams(
                 collective_id=0, has_side_effects=True, vmem_limit_bytes=67043328
             ),
-        )(x, meta, w_gate, w_up, w_down)
+        )(x, expert.T, slot.T, gate.T, w_gate, w_up, w_down)
+        y = pl.pallas_call(
+            end_kernel,
+            out_shape=jax.ShapeDtypeStruct((tokens, d), BF),
+            in_specs=[any_] * 3,
+            out_specs=any_,
+            scratch_shapes=[
+                pltpu.VMEM((tokens, d - BC), BF),
+                pltpu.VMEM((2, tokens, BC), BF),
+                pltpu.VMEM((tokens, BC), F32),
+                pltpu.VMEM((tokens, BC), BF),
+                dma((PIECES,)),
+                dma((PIECES,)),
+                dma((3,)),
+            ],
+            compiler_params=pltpu.CompilerParams(vmem_limit_bytes=67043328),
+        )(y, last, own)
         return y[None, None]
 
     token, weight = P("dp", "ep", None, None), P("ep", None, None)

time: 176 us -> 172 us (0.977)
  local copies, waits for them, and re-layouts: 3.16 us -> 0 us
  other arithmetic: 2.08 us -> 0 us
    unnamed x1 -> x0, local copies, waits for them, and re-layouts: 3.16 us -> none
    pallas_call x0 -> x1, Pallas kernels: none -> 3.1 us  [step(): pl.pallas_call(end_kernel, out_shape=jax.ShapeDtypeStruct((tokens, d), BF...]
    pallas_call x1, Pallas kernels: 171 us -> 168 us  [step(): pl.pallas_call(functools.partial(kernel, n, el, cap), out_shape=[jax.Shap...]
where the time goes in v3:
time: 172 us; the launch traced here: 171 us
  Pallas kernels  171 us (99%)
    pallas_call x1, Pallas kernels, step(): pl.pallas_call(functools.partial(kernel, n, el, cap), out_shape=[jax.Shap...  168 us

profile of v3, /device:TPU:112, one launch (start us, length us, event | category | flops | bytes accessed | tf_op | source)
XLA Modules:
  0.0 171.5 jit_solution(15138384887448175246)
XLA Ops:
  0.0 168.4 %shard_map.73 = (bf16[512,1792]{1,0:T(8,128)(2,1)}, bf16[7,2,512,256]{3,2,1,0:T(8,128)(2,1)}, bf16[2,512,256]{2,1,0:T(8,128)(2,1)}, f32[512,256]{1,0:T(8,128)}) custom-call(bf16[512,2048]{1,0:T(8,128)(2,1)} %bitcast.11, s32[8,512]{1,0:T(8,128)} %bitcast.12, s32[8,512]{1,0:T(8,128)} %bitcast.13, f32[8,512]{1,0:T(8,128)} %bitcast.14, ...), custom_call_target="tpu_custom_call" | custom-call | tf_op jit(solution)/shard_map/pallas_call | solution.py:460
  168.4 3.1 %shard_map.74 = bf16[512,2048]{1,0:T(8,128)(2,1)} custom-call(bf16[512,1792]{1,0:T(8,128)(2,1)} %get-tuple-element.8.most_ref, bf16[2,512,256]{2,1,0:T(8,128)(2,1)} %get-tuple-element.9.last_ref, f32[512,256]{1,0:T(8,128)} %get-tuple-element.10.own_ref), custom_call_target="tpu_custom_call" | custom-call | tf_op jit(solution)/shard_map/pallas_call | solution.py:499

commit v4 on v3

--- a/solution.py
+++ b/solution.py
@@ -39,7 +39,10 @@
     def start_gu(c, e):
         for i, w in enumerate((wg_ref, wu_ref)):
             s = lax.rem(c * (2 * el) + 2 * e + i, NB)
-            pltpu.make_async_copy(w.at[e, pl.ds(c * BC, BC)], wbuf.at[s], wsem.at[s]).start()
+            for j in range(2):
+                pltpu.make_async_copy(
+                    w.at[e, pl.ds(c * BC + j * (BC // 2), BC // 2)], wbuf.at[s, pl.ds(j * (BC // 2), BC // 2)], wsem.at[s]
+                ).start()
 
     def start_dn(c, e):
         s = lax.rem(tiles1 + c * el + e, NB)
@@ -430,16 +433,16 @@
     rows = [pl.ds(i * (tokens // PIECES), tokens // PIECES) for i in range(PIECES)]
     ins = [pltpu.make_async_copy(most_ref.at[r], most.at[r], in_sem.at[i]) for i, r in enumerate(rows)]
     outs = [pltpu.make_async_copy(most.at[r], y_ref.at[r, pl.ds(0, width)], out_sem.at[i]) for i, r in enumerate(rows)]
-    for c in lasts + ins:
+    for c in ins + lasts:
         c.start()
+    for i, o in zip(ins, outs):
+        i.wait()
+        o.start()
     for c in lasts:
         c.wait()
     end[...] = (own[...] + last[0].astype(F32) + last[1].astype(F32)).astype(BF)
     final = pltpu.make_async_copy(end, y_ref.at[:, pl.ds(width, end.shape[1])], sem.at[2])
     final.start()
-    for i, o in zip(ins, outs):
-        i.wait()
-        o.start()
     for o in outs:
         o.wait()
     final.wait()

time: 172 us -> 171 us (level)
  no operation moved by 1% of the time
where the time goes in v4:
time: 171 us
  Pallas kernels  171 us (100%)
    pallas_call x1, Pallas kernels, step(): pl.pallas_call(functools.partial(kernel, n, el, cap), out_shape=[jax.Shap...  168 us

profile of v4, /device:TPU:112, one launch (start us, length us, event | category | flops | bytes accessed | tf_op | source)
XLA Modules:
  0.0 171.0 jit_solution(13823717321940677162)
XLA Ops:
  0.0 168.4 %shard_map.73 = (bf16[512,1792]{1,0:T(8,128)(2,1)}, bf16[7,2,512,256]{3,2,1,0:T(8,128)(2,1)}, bf16[2,512,256]{2,1,0:T(8,128)(2,1)}, f32[512,256]{1,0:T(8,128)}) custom-call(bf16[512,2048]{1,0:T(8,128)(2,1)} %bitcast.11, s32[8,512]{1,0:T(8,128)} %bitcast.12, s32[8,512]{1,0:T(8,128)} %bitcast.13, f32[8,512]{1,0:T(8,128)} %bitcast.14, ...), custom_call_target="tpu_custom_call" | custom-call | tf_op jit(solution)/shard_map/pallas_call | solution.py:463
  168.4 2.6 %shard_map.74 = bf16[512,2048]{1,0:T(8,128)(2,1)} custom-call(bf16[512,1792]{1,0:T(8,128)(2,1)} %get-tuple-element.8.most_ref, bf16[2,512,256]{2,1,0:T(8,128)(2,1)} %get-tuple-element.9.last_ref, f32[512,256]{1,0:T(8,128)} %get-tuple-element.10.own_ref), custom_call_target="tpu_custom_call" | custom-call | tf_op jit(solution)/shard_map/pallas_call | solution.py:502
